TPU v7x, 32 devices: a whole 2x2x4 slice. The times are simulated.
32 devices in a mesh: dp: 16 (over z, y, core), tensor: 2 (over x).
Axes of the slice: x: 2, y: 2, z: 4, core: 2. Of those that a mesh axis runs over, the one named last changes fastest.
Arguments:
- tokens: bfloat16 [64, 144, 1024], P('dp', 'tensor'), may hold values from -150 to 150
- cotangent: bfloat16 [64, 144, 1024], P('dp', 'tensor'), may hold values from -6 to 6
- dispatch_weight: bfloat16 [1024, 32], replicated, may hold values from -3 to 3
- w_in: bfloat16 [32, 1024, 4096], P('dp', None, 'tensor'), may hold values from -0.1875 to 0.1875
- w_out: bfloat16 [32, 4096, 1024], P('dp', 'tensor'), may hold values from -0.09375 to 0.09375
Outputs:
- grad_tokens: bfloat16 [64, 144, 1024], P('dp', 'tensor')
- grad_router: float32 [1024, 32], replicated
- grad_w_in: bfloat16 [32, 1024, 4096], P('dp', None, 'tensor')
- grad_w_out: bfloat16 [32, 4096, 1024], P('dp', 'tensor')
All inputs are finite; a program needn't handle non-finite values.
Results may differ from a plain program's by a relative error of at most 0.0079.
Values may be sent and summed in bfloat16 or wider, within the bound.
A program may use at most 64 MiB of HBM per device.

v0:
```python
import jax
import jax.numpy as jnp
from jax import lax
from jax.sharding import PartitionSpec as P


def to_experts(partial_rows):
    shared_part = lax.psum_scatter(partial_rows, "tensor", scatter_dimension=2, tiled=True).astype(
        jnp.bfloat16
    )
    arrived = lax.all_to_all(shared_part, "dp", split_axis=1, concat_axis=0, tiled=True)
    result = lax.all_gather(arrived, "tensor", axis=2, tiled=True)
    return result


def to_images(partial_rows):
    shared_part = lax.psum_scatter(partial_rows, "tensor", scatter_dimension=2, tiled=True).astype(
        jnp.bfloat16
    )
    arrived = lax.all_to_all(shared_part, "dp", split_axis=0, concat_axis=1, tiled=True)
    result = lax.all_gather(arrived, "tensor", axis=2, tiled=True)
    return result


def dispatch_softmax(logits):
    local_max = jnp.max(logits, axis=1)
    global_max = lax.pmax(local_max, "tensor")
    exponent = jnp.exp(logits - global_max[:, None, :])
    totals = lax.psum(jnp.sum(exponent, axis=1), "tensor")
    return exponent / totals[:, None, :]


def on_device(tokens, cotangent, dispatch_weight, w_in, w_out):
    wide = jnp.float32
    logits = jnp.einsum("isd,de->ise", tokens, dispatch_weight, preferred_element_type=wide)
    dispatch = dispatch_softmax(logits)
    combine = jax.nn.softmax(logits, axis=2)
    dispatch_low = dispatch.astype(jnp.bfloat16)
    combine_low = combine.astype(jnp.bfloat16)
    slot_inputs = to_experts(
        jnp.einsum("ise,isd->ied", dispatch_low, tokens, preferred_element_type=wide)
    )
    pre_act = jnp.einsum("ied,edf->ief", slot_inputs, w_in, preferred_element_type=wide)
    hidden_act, gelu_back = jax.vjp(jax.nn.gelu, pre_act)
    hidden_low = hidden_act.astype(jnp.bfloat16)
    slot_outputs = to_images(
        jnp.einsum("ief,efd->ied", hidden_low, w_out, preferred_element_type=wide)
    )
    grad_combine = jnp.einsum("isd,ied->ise", cotangent, slot_outputs, preferred_element_type=wide)
    grad_slots_out = to_experts(
        jnp.einsum("ise,isd->ied", combine_low, cotangent, preferred_element_type=wide)
    )
    grad_hidden = jnp.einsum("ied,efd->ief", grad_slots_out, w_out, preferred_element_type=wide)
    grad_pre = gelu_back(grad_hidden)[0].astype(jnp.bfloat16)
    grad_w_out = jnp.einsum(
        "ief,ied->efd", hidden_low, grad_slots_out, preferred_element_type=wide
    ).astype(jnp.bfloat16)
    grad_w_in = jnp.einsum(
        "ied,ief->edf", slot_inputs, grad_pre, preferred_element_type=wide
    ).astype(jnp.bfloat16)
    grad_slots_in = to_images(
        jnp.einsum("ief,edf->ied", grad_pre, w_in, preferred_element_type=wide)
    )
    grad_dispatch = jnp.einsum("isd,ied->ise", tokens, grad_slots_in, preferred_element_type=wide)
    column_dot = lax.psum(jnp.sum(grad_dispatch * dispatch, axis=1), "tensor")
    row_dot = jnp.sum(grad_combine * combine, axis=2, keepdims=True)
    grad_logits = (
        combine * (grad_combine - row_dot) + dispatch * (grad_dispatch - column_dot[:, None, :])
    ).astype(jnp.bfloat16)
    token_part = jnp.einsum(
        "ise,ied->isd", dispatch_low, grad_slots_in, preferred_element_type=wide
    )
    router_part = jnp.einsum(
        "ise,de->isd", grad_logits, dispatch_weight, preferred_element_type=wide
    )
    grad_tokens = (token_part + router_part).astype(jnp.bfloat16)
    local_router = jnp.einsum("isd,ise->de", tokens, grad_logits, preferred_element_type=wide)
    grad_router = lax.psum(local_router, ("dp", "tensor"))
    return (grad_tokens, grad_router, grad_w_in, grad_w_out)


def solution(mesh):
    return jax.shard_map(
        on_device,
        mesh=mesh,
        in_specs=(
            P("dp", "tensor", None),
            P("dp", "tensor", None),
            P(),
            P("dp", None, "tensor"),
            P("dp", "tensor", None),
        ),
        out_specs=(P("dp", "tensor", None), P(), P("dp", None, "tensor"), P("dp", "tensor", None)),
        check_vma=False,
    )
```

profile of v0, /device:TPU:0, one launch (start us, length us, event | category | flops | bytes accessed | tf_op | source)
XLA Modules:
  0.0 270.4 jit_solution(4491643558524088509)
XLA Ops:
  7.2 1.0 copy-done
  8.2 1.3 fusion.37
  9.5 0.2 fusion.38
  9.7 2.1 fusion.26
  11.8 0.0 reduce-scatter.7.cloned.1.call-start
  11.9 5.9 %pmax.7 = f32[4,32]{1,0:T(4,128)S(1)} all-reduce(f32[4,32]{1,0:T(4,128)S(1)} %get-tuple-element.4), channel_id=1, replica_groups=mesh['dp'=16,'tensor'=2] {'tensor'}, use_global_device_ids=true, to_apply=%region_1.0 | all-reduce | flops 128 | bytes 1024 | tf_op jit(solution)/shard_map/pmax | solution.py:27
  17.7 0.2 fusion.25
  17.9 4.9 %psum.21 = f32[4,32]{1,0:T(4,128)S(1)} all-reduce(f32[4,32]{1,0:T(4,128)S(1)} %fusion.25), channel_id=1, replica_groups=mesh['dp'=16,'tensor'=2] {'tensor'}, use_global_device_ids=true, to_apply=%region_3.0 | all-reduce | flops 128 | bytes 1024 | tf_op jit(solution)/shard_map/psum | solution.py:29
  22.9 1.1 fusion.29
  24.0 5.4 %reduce-scatter.5.cloned.1.call-done = f32[4,32,512]{2,1,0:T(8,128)} async-done(((f32[4,32,1024]{2,1,0:T(8,128)}), f32[4,32,512]{2,1,0:T(8,128)}) %reduce-scatter.5.cloned.1.call-update) | async-done | bytes 262160 | tf_op jit(solution)/shard_map/reduce_scatter | solution.py:8
  29.4 1.0 convert_element_type.38
  30.3 0.8 copy.13
  31.1 5.6 %all-to-all-start = ((bf16[4,32,512]{2,0,1:T(4,128)(2,1)}), bf16[4,32,512]{2,0,1:T(4,128)(2,1)S(1)}, u32[]{:S(2)}, u32[]{:S(2)}) async-start(bf16[4,32,512]{2,0,1:T(4,128)(2,1)} %copy.13), calls=%async_computation.1 | async-start | bytes 262144 | tf_op jit(solution)/shard_map/all_to_all | solution.py:11
  36.7 10.1 %reduce-scatter.7.cloned.1.call-done = f32[4,32,512]{2,1,0:T(8,128)} async-done(((f32[4,32,1024]{2,1,0:T(8,128)}), f32[4,32,512]{2,1,0:T(8,128)}) %reduce-scatter.7.cloned.1.call-update) | async-done | bytes 262160 | tf_op jit(solution)/shard_map/reduce_scatter | solution.py:8
  46.9 1.0 convert_element_type.39
  47.8 0.8 copy.15
  48.6 5.6 %all-to-all-start.1 = ((bf16[4,32,512]{2,0,1:T(4,128)(2,1)}), bf16[4,32,512]{2,0,1:T(4,128)(2,1)S(1)}, u32[]{:S(2)}, u32[]{:S(2)}) async-start(bf16[4,32,512]{2,0,1:T(4,128)(2,1)} %copy.15), calls=%async_computation.3 | async-start | bytes 262144 | tf_op jit(solution)/shard_map/all_to_all | solution.py:11
  54.4 6.5 %all_gather.12 = bf16[64,2,1024]{2,0,1:T(8,128)(2,1)S(1)} all-gather(bf16[64,2,512]{2,0,1:T(8,128)(2,1)S(1)} %all_to_all.55), channel_id=1, replica_groups=mesh['dp'=16,'tensor'=2] {'tensor'}, dimensions={2}, use_global_device_ids=true | all-gather | bytes 393216 | tf_op jit(solution)/shard_map/all_gather | solution.py:12
  60.8 1.3 all-to-all-done.1
  62.2 5.8 %all_gather.13 = bf16[64,2,1024]{2,0,1:T(8,128)(2,1)S(1)} all-gather(bf16[64,2,512]{2,0,1:T(8,128)(2,1)S(1)} %all_to_all.59), channel_id=1, replica_groups=mesh['dp'=16,'tensor'=2] {'tensor'}, dimensions={2}, use_global_device_ids=true | all-gather | bytes 393216 | tf_op jit(solution)/shard_map/all_gather | solution.py:12
  68.0 5.1 %convolution_bitcast_fusion = f32[64,2,2048]{2,0,1:T(8,128)S(1)} fusion(bf16[64,2,1024]{2,0,1:T(8,128)(2,1)S(1)} %all_gather.13, bf16[2,1024,2048]{2,1,0:T(8,128)(2,1)} %param.8), kind=kOutput, calls=%fused_computation.4 | convolution fusion | flops 536870912 | bytes 9699328 | tf_op jit(solution)/shard_map/ied,edf->ief/dot_general | solution.py:43
  73.1 2.9 %fusion.16 = bf16[64,2,2048]{2,0,1:T(8,128)(2,1)S(1)} fusion(f32[64,2,2048]{2,0,1:T(8,128)S(1)} %convolution_bitcast_fusion, bf16[64,2,1024]{2,0,1:T(8,128)(2,1)S(1)} %all_gather.12, bf16[2,2048,1024]{2,1,0:T(8,128)(2,1)S(1)} %copy-done.1), kind=kOutput, calls=%fused_computation.28 | convolution fusion | flops 542113792 | bytes 10223616 | tf_op jit(solution)/shard_map/ied,efd->ief/dot_general | solution.py:53
  76.0 3.5 %convolution_bitcast_fusion.3 = f32[64,2,1024]{2,0,1:T(8,128)} fusion(bf16[64,2,2048]{2,0,1:T(8,128)(2,1)S(1)} %fusion.16, bf16[2,1024,2048]{2,1,0:T(8,128)(2,1)S(1)} %bitcast.67), kind=kOutput, calls=%fused_computation.11 | convolution fusion | flops 536870912 | bytes 9437184 | tf_op jit(solution)/shard_map/ief,edf->ied/dot_general | solution.py:62
  79.6 5.7 %convolution_bitcast_fusion.2 = f32[64,2,1024]{2,0,1:T(8,128)} fusion(bf16[2,2048,1024]{2,1,0:T(8,128)(2,1)} %param.9, f32[64,2,2048]{2,0,1:T(8,128)S(1)} %convolution_bitcast_fusion), kind=kOutput, calls=%fused_computation.10 | convolution fusion | flops 539230208 | bytes 9961472 | tf_op jit(solution)/shard_map/ief,efd->ied/dot_general | solution.py:47
  85.3 5.8 %convolution_convert_fusion = bf16[2,2048,1024]{2,1,0:T(8,128)(2,1)} fusion(bf16[64,2,1024]{2,0,1:T(8,128)(2,1)S(1)} %all_gather.12, f32[64,2,2048]{2,0,1:T(8,128)S(1)} %convolution_bitcast_fusion), kind=kOutput, calls=%fused_computation.2 | convolution fusion | flops 543424512 | bytes 9699328 | tf_op jit(solution)/shard_map/ief,ied->efd/dot_general | solution.py:55
  91.1 2.0 reduce-scatter.9.cloned.1.call-done
  93.1 1.0 convert_element_type.41
  94.1 0.8 copy.17
  94.9 5.6 %all-to-all-start.2 = ((bf16[64,2,512]{2,1,0:T(2,128)(2,1)}), bf16[64,2,512]{2,1,0:T(2,128)(2,1)S(1)}, u32[]{:S(2)}, u32[]{:S(2)}) async-start(bf16[64,2,512]{2,1,0:T(2,128)(2,1)} %copy.17), calls=%async_computation.5 | async-start | bytes 262144 | tf_op jit(solution)/shard_map/all_to_all | solution.py:20
  100.5 5.8 %convolution_convert_fusion.1 = bf16[2,1024,2048]{2,1,0:T(8,128)(2,1)} fusion(bf16[64,2,1024]{2,0,1:T(8,128)(2,1)S(1)} %all_gather.13, bf16[64,2,2048]{2,0,1:T(8,128)(2,1)S(1)} %fusion.16), kind=kOutput, calls=%fused_computation.3 | convolution fusion | flops 541065216 | bytes 9175040 | tf_op jit(solution)/shard_map/ied,ief->edf/dot_general | solution.py:58
  106.3 4.2 %reduce-scatter.11.cloned.1.call-done = f32[64,2,512]{2,0,1:T(8,128)} async-done(((f32[64,2,1024]{2,0,1:T(8,128)}), f32[64,2,512]{2,0,1:T(8,128)}) %reduce-scatter.11.cloned.1.call-update) | async-done | bytes 262160 | tf_op jit(solution)/shard_map/reduce_scatter | solution.py:17
  110.4 1.0 convert_element_type.43
  111.4 0.8 copy.19
  112.2 5.6 %all-to-all-start.3 = ((bf16[64,2,512]{2,1,0:T(2,128)(2,1)}), bf16[64,2,512]{2,1,0:T(2,128)(2,1)S(1)}, u32[]{:S(2)}, u32[]{:S(2)}) async-start(bf16[64,2,512]{2,1,0:T(2,128)(2,1)} %copy.19), calls=%async_computation.7 | async-start | bytes 262144 | tf_op jit(solution)/shard_map/all_to_all | solution.py:20
  117.9 0.1 copy.26
  118.0 0.1 all_to_all.63
  118.1 6.5 %all_gather.14 = bf16[4,32,1024]{2,1,0:T(8,128)(2,1)S(1)} all-gather(bf16[4,32,512]{2,1,0:T(8,128)(2,1)S(1)} %all_to_all.63), channel_id=1, replica_groups=mesh['dp'=16,'tensor'=2] {'tensor'}, dimensions={2}, use_global_device_ids=true | all-gather | bytes 393216 | tf_op jit(solution)/shard_map/all_gather | solution.py:21
  124.5 0.4 multiply_reduce_fusion.1
  124.9 4.9 %psum.22 = f32[4,32]{1,0:T(4,128)S(1)} all-reduce(f32[4,32]{1,0:T(4,128)S(1)} %get-tuple-element.8), channel_id=1, replica_groups=mesh['dp'=16,'tensor'=2] {'tensor'}, use_global_device_ids=true, to_apply=%region_12.0 | all-reduce | flops 128 | bytes 1024 | tf_op jit(solution)/shard_map/psum | solution.py:65
  129.9 0.1 copy.25
  129.9 0.1 all_to_all.67
  130.0 5.6 %all_gather.15 = bf16[4,32,1024]{2,1,0:T(8,128)(2,1)S(1)} all-gather(bf16[4,32,512]{2,1,0:T(8,128)(2,1)S(1)} %all_to_all.67), channel_id=1, replica_groups=mesh['dp'=16,'tensor'=2] {'tensor'}, dimensions={2}, use_global_device_ids=true | all-gather | bytes 393216 | tf_op jit(solution)/shard_map/all_gather | solution.py:21
  135.7 0.3 convolution_bitcast_fusion.6
  135.9 1.0 convolution_bitcast_fusion.4
  137.0 0.4 fusion.9
  137.5 1.3 fusion.2
  138.7 123.5 %all-reduce.2.cloned.1.call-done = f32[1024,32]{0,1:T(8,128)} async-done(((f32[1024,32]{0,1:T(8,128)}), f32[1024,32]{0,1:T(8,128)}) %all-reduce.2.cloned.1.call-update) | async-done | bytes 131088 | tf_op jit(solution)/shard_map/psum | solution.py:78
  262.3 1.6 copy.30
  (28 shorter events, 0.5 us)
Async XLA Ops:
  7.2 1.1 copy-start
  7.2 22.2 %reduce-scatter.5.cloned.1.call-start = ((), (), s32[]{:S(2)}) async-start(), calls=%async_computation.8 | async-start | bytes 786432 | tf_op jit(solution)/shard_map/reduce_scatter | solution.py:8
  11.8 35.0 %reduce-scatter.7.cloned.1.call-start = ((), (), s32[]{:S(2)}) async-start(), calls=%async_computation.9 | async-start | bytes 786432 | tf_op jit(solution)/shard_map/reduce_scatter | solution.py:8
  31.1 17.5 %all-to-all-start = ((bf16[4,32,512]{2,0,1:T(4,128)(2,1)}), bf16[4,32,512]{2,0,1:T(4,128)(2,1)S(1)}, u32[]{:S(2)}, u32[]{:S(2)}) async-start(bf16[4,32,512]{2,0,1:T(4,128)(2,1)} %copy.13), calls=%async_computation.1 | async-start | bytes 262144 | tf_op jit(solution)/shard_map/all_to_all | solution.py:11
  48.6 13.5 %all-to-all-start.1 = ((bf16[4,32,512]{2,0,1:T(4,128)(2,1)}), bf16[4,32,512]{2,0,1:T(4,128)(2,1)S(1)}, u32[]{:S(2)}, u32[]{:S(2)}) async-start(bf16[4,32,512]{2,0,1:T(4,128)(2,1)} %copy.15), calls=%async_computation.3 | async-start | bytes 262144 | tf_op jit(solution)/shard_map/all_to_all | solution.py:11
  54.2 38.9 %reduce-scatter.9.cloned.1.call-start = ((), (), s32[]{:S(2)}) async-start(), calls=%async_computation.10 | async-start | bytes 786432 | tf_op jit(solution)/shard_map/reduce_scatter | solution.py:17
  62.2 10.9 %copy-start.1 = (bf16[2,2048,1024]{2,1,0:T(8,128)(2,1)S(1)}, bf16[2,2048,1024]{2,1,0:T(8,128)(2,1)}, u32[]{:S(2)}) copy-start(bf16[2,2048,1024]{2,1,0:T(8,128)(2,1)} %param.9) | copy-start | bytes 25165828
  62.2 13.8 %slice-start = ((s8[8388608]{0:T(1024)(128)(4,1)}), s8[4194304]{0:T(1024)(128)(4,1)S(1)}, s32[]{:S(2)}) async-start(s8[8388608]{0:T(1024)(128)(4,1)} %bitcast.66), calls=%async_computation.13 | async-start | bytes 8388608
  68.0 8.0 %slice-start.1 = ((s8[8388608]{0:T(1024)(128)(4,1)}), s8[4194304]{0:T(1024)(128)(4,1)S(1)}, s32[]{:S(2)}) async-start(s8[8388608]{0:T(1024)(128)(4,1)} %bitcast.66), calls=%async_computation.14 | async-start | bytes 8388608
  79.5 30.9 %reduce-scatter.11.cloned.1.call-start = ((), (), s32[]{:S(2)}) async-start(), calls=%async_computation.11 | async-start | bytes 786432 | tf_op jit(solution)/shard_map/reduce_scatter | solution.py:17
  91.1 44.6 %copy-start.2 = (bf16[4,72,1024]{2,1,0:T(8,128)(2,1)S(1)}, bf16[4,72,1024]{2,1,0:T(8,128)(2,1)}, u32[]{:S(2)}) copy-start(bf16[4,72,1024]{2,1,0:T(8,128)(2,1)} %param.6) | copy-start | bytes 1769476
  91.1 45.9 %copy-start.3 = (bf16[1024,32]{0,1:T(8,128)(2,1)S(1)}, bf16[1024,32]{0,1:T(8,128)(2,1)}, u32[]{:S(2)}) copy-start(bf16[1024,32]{0,1:T(8,128)(2,1)} %param.7) | copy-start | bytes 196612
  94.9 17.3 %all-to-all-start.2 = ((bf16[64,2,512]{2,1,0:T(2,128)(2,1)}), bf16[64,2,512]{2,1,0:T(2,128)(2,1)S(1)}, u32[]{:S(2)}, u32[]{:S(2)}) async-start(bf16[64,2,512]{2,1,0:T(2,128)(2,1)} %copy.17), calls=%async_computation.5 | async-start | bytes 262144 | tf_op jit(solution)/shard_map/all_to_all | solution.py:20
  112.2 17.6 %all-to-all-start.3 = ((bf16[64,2,512]{2,1,0:T(2,128)(2,1)}), bf16[64,2,512]{2,1,0:T(2,128)(2,1)S(1)}, u32[]{:S(2)}, u32[]{:S(2)}) async-start(bf16[64,2,512]{2,1,0:T(2,128)(2,1)} %copy.19), calls=%async_computation.7 | async-start | bytes 262144 | tf_op jit(solution)/shard_map/all_to_all | solution.py:20
  117.9 144.4 %all-reduce.2.cloned.1.call-start = ((), (), s32[]{:S(2)}) async-start(), calls=%async_computation.12 | async-start | bytes 262144 | tf_op jit(solution)/shard_map/psum | solution.py:78
Sparse Core Ops, SparseCore 0:
  11.9 17.3 reduce-scatter.4
  32.2 14.6 reduce-scatter.6
  79.6 13.4 reduce-scatter.8
  95.8 14.6 reduce-scatter.10
  137.6 124.6 all-reduce.1
where the time goes:
time: 271 us; the launch traced here: 270 us
  waiting for transfers between devices  147 us (54%)
  blocking collectives  40.1 us (15%)
  matrix products  36.6 us (14%)
  starting transfers between devices  22.7 us (8%)
  between operations  14 us (5%)
  local copies, waits for them, and re-layouts  6.18 us (2%)
  other arithmetic  4.2 us (2%)
    psum x1, waiting for transfers between devices, on_device(): grad_router = lax.psum(local_router, ('dp', 'tensor'))  124 us
    reduce_scatter x2, waiting for transfers between devices, to_experts(): lax.psum_scatter(partial_rows, 'tensor', scatter_dimension=2, tiled=True)  15.5 us
    all_gather x2, blocking collectives, to_experts(): result = lax.all_gather(arrived, 'tensor', axis=2, tiled=True)  12.2 us
    all_gather x2, blocking collectives, to_images(): result = lax.all_gather(arrived, 'tensor', axis=2, tiled=True)  12.1 us
    all_to_all x2, starting transfers between devices, to_images(): lax.all_to_all(shared_part, 'dp', split_axis=0, concat_axis=1, tiled=True)  11.3 us
    all_to_all x2, starting transfers between devices, to_experts(): lax.all_to_all(shared_part, 'dp', split_axis=1, concat_axis=0, tiled=True)  11.2 us
    reduce_scatter x2, waiting for transfers between devices, to_images(): lax.psum_scatter(partial_rows, 'tensor', scatter_dimension=2, tiled=True)  6.15 us
    pmax x1, blocking collectives, dispatch_softmax(): global_max = lax.pmax(local_max, 'tensor')  5.87 us
  transfers between devices with their start and end apart: 9, of which 6 were waited for; matrix products, arithmetic and copies ran while one was open for 10% of the time, Pallas kernels for 0%

commit v1 on v0

--- a/solution.py
+++ b/solution.py
@@ -75,7 +75,7 @@
     )
     grad_tokens = (token_part + router_part).astype(jnp.bfloat16)
     local_router = jnp.einsum("isd,ise->de", tokens, grad_logits, preferred_element_type=wide)
-    grad_router = lax.psum(local_router, ("dp", "tensor"))
+    grad_router = jnp.sum(lax.all_gather(local_router, ("dp", "tensor")), axis=0)
     return (grad_tokens, grad_router, grad_w_in, grad_w_out)
 
 

time: 271 us -> 217 us (0.80)
  waiting for transfers between devices: 147 us -> 82.9 us
  local copies, waits for them, and re-layouts: 6.18 us -> 11.7 us
    psum x1 -> x0, waiting for transfers between devices: 124 us -> none  [on_device(): grad_router = lax.psum(local_router, ('dp', 'tensor'))]
    all_gather x0 -> x1, waiting for transfers between devices: none -> 48.4 us  [on_device(): lax.all_gather(local_router, ('dp', 'tensor'))]
    reduce_scatter x2, waiting for transfers between devices: 6.15 us -> 17.7 us  [to_images(): lax.psum_scatter(partial_rows, 'tensor', scatter_dimension=2, tiled=True)]
    unnamed x13 -> x17, local copies, waits for them, and re-layouts: 2.61 us -> 5.67 us
  transfers between devices with their start and end apart: 9 -> 9, of which waited for: 6 -> 6; matrix products, arithmetic and copies ran while one was open for 10% -> 13% of each run, Pallas kernels for 0% -> 0%
where the time goes in v1:
time: 217 us; the launch traced here: 216 us
  waiting for transfers between devices  82.9 us (38%)
  blocking collectives  40.2 us (19%)
  matrix products  38.5 us (18%)
  starting transfers between devices  22.8 us (11%)
  between operations  14 us (6%)
  local copies, waits for them, and re-layouts  11.7 us (5%)
  other arithmetic  5.95 us (3%)
    all_gather x1, waiting for transfers between devices, on_device(): lax.all_gather(local_router, ('dp', 'tensor'))  48.4 us
    reduce_scatter x2, waiting for transfers between devices, to_images(): lax.psum_scatter(partial_rows, 'tensor', scatter_dimension=2, tiled=True)  17.7 us
    reduce_scatter x2, waiting for transfers between devices, to_experts(): lax.psum_scatter(partial_rows, 'tensor', scatter_dimension=2, tiled=True)  15.5 us
    all_gather x2, blocking collectives, to_experts(): result = lax.all_gather(arrived, 'tensor', axis=2, tiled=True)  12.2 us
    all_gather x2, blocking collectives, to_images(): result = lax.all_gather(arrived, 'tensor', axis=2, tiled=True)  12.2 us
    all_to_all x2, starting transfers between devices, to_images(): lax.all_to_all(shared_part, 'dp', split_axis=0, concat_axis=1, tiled=True)  11.3 us
    all_to_all x2, starting transfers between devices, to_experts(): lax.all_to_all(shared_part, 'dp', split_axis=1, concat_axis=0, tiled=True)  11.2 us
    pmax x1, blocking collectives, dispatch_softmax(): global_max = lax.pmax(local_max, 'tensor')  5.87 us
  transfers between devices with their start and end apart: 9, of which 6 were waited for; matrix products, arithmetic and copies ran while one was open for 13% of the time, Pallas kernels for 0%

profile of v1, /device:TPU:0, one launch (start us, length us, event | category | flops | bytes accessed | tf_op | source)
XLA Modules:
  0.0 216.1 jit_solution(2641665952350378834)
XLA Ops:
  7.2 1.0 copy-done
  8.2 1.3 fusion.37
  9.5 0.6 fusion.38
  10.2 2.1 fusion.26
  12.4 5.9 %pmax.7 = f32[4,32]{1,0:T(4,128)S(1)} all-reduce(f32[4,32]{1,0:T(4,128)S(1)} %get-tuple-element.4), channel_id=1, replica_groups=mesh['dp'=16,'tensor'=2] {'tensor'}, use_global_device_ids=true, to_apply=%region_1.0 | all-reduce | flops 128 | bytes 1024 | tf_op jit(solution)/shard_map/pmax | solution.py:27
  18.2 0.2 fusion.25
  18.4 4.9 %psum.14 = f32[4,32]{1,0:T(4,128)S(1)} all-reduce(f32[4,32]{1,0:T(4,128)S(1)} %fusion.25), channel_id=1, replica_groups=mesh['dp'=16,'tensor'=2] {'tensor'}, use_global_device_ids=true, to_apply=%region_3.0 | all-reduce | flops 128 | bytes 1024 | tf_op jit(solution)/shard_map/psum | solution.py:29
  23.3 1.1 fusion.29
  24.5 5.4 %reduce-scatter.5.cloned.1.call-done = f32[4,32,512]{2,1,0:T(8,128)} async-done(((f32[4,32,1024]{2,1,0:T(8,128)}), f32[4,32,512]{2,1,0:T(8,128)}) %reduce-scatter.5.cloned.1.call-update) | async-done | bytes 262160 | tf_op jit(solution)/shard_map/reduce_scatter | solution.py:8
  29.8 1.0 convert_element_type.38
  30.8 0.8 copy.13
  31.6 5.6 %all-to-all-start = ((bf16[4,32,512]{2,0,1:T(4,128)(2,1)}), bf16[4,32,512]{2,0,1:T(4,128)(2,1)S(1)}, u32[]{:S(2)}, u32[]{:S(2)}) async-start(bf16[4,32,512]{2,0,1:T(4,128)(2,1)} %copy.13), calls=%async_computation.1 | async-start | bytes 262144 | tf_op jit(solution)/shard_map/all_to_all | solution.py:11
  37.2 10.1 %reduce-scatter.7.cloned.1.call-done = f32[4,32,512]{2,1,0:T(8,128)} async-done(((f32[4,32,1024]{2,1,0:T(8,128)}), f32[4,32,512]{2,1,0:T(8,128)}) %reduce-scatter.7.cloned.1.call-update) | async-done | bytes 262160 | tf_op jit(solution)/shard_map/reduce_scatter | solution.py:8
  47.3 1.0 convert_element_type.39
  48.3 0.8 copy.15
  49.1 5.6 %all-to-all-start.1 = ((bf16[4,32,512]{2,0,1:T(4,128)(2,1)}), bf16[4,32,512]{2,0,1:T(4,128)(2,1)S(1)}, u32[]{:S(2)}, u32[]{:S(2)}) async-start(bf16[4,32,512]{2,0,1:T(4,128)(2,1)} %copy.15), calls=%async_computation.3 | async-start | bytes 262144 | tf_op jit(solution)/shard_map/all_to_all | solution.py:11
  54.8 6.5 %all_gather.18 = bf16[64,2,1024]{2,0,1:T(8,128)(2,1)S(1)} all-gather(bf16[64,2,512]{2,0,1:T(8,128)(2,1)S(1)} %all_to_all.55), channel_id=1, replica_groups=mesh['dp'=16,'tensor'=2] {'tensor'}, dimensions={2}, use_global_device_ids=true | all-gather | bytes 393216 | tf_op jit(solution)/shard_map/all_gather | solution.py:12
  61.3 1.3 all-to-all-done.1
  62.7 5.8 %all_gather.19 = bf16[64,2,1024]{2,0,1:T(8,128)(2,1)S(1)} all-gather(bf16[64,2,512]{2,0,1:T(8,128)(2,1)S(1)} %all_to_all.59), channel_id=1, replica_groups=mesh['dp'=16,'tensor'=2] {'tensor'}, dimensions={2}, use_global_device_ids=true | all-gather | bytes 393216 | tf_op jit(solution)/shard_map/all_gather | solution.py:12
  68.5 5.1 %convolution_bitcast_fusion = f32[64,2,2048]{2,0,1:T(8,128)S(1)} fusion(bf16[64,2,1024]{2,0,1:T(8,128)(2,1)S(1)} %all_gather.19, bf16[2,1024,2048]{2,1,0:T(8,128)(2,1)} %param.8), kind=kOutput, calls=%fused_computation.5 | convolution fusion | flops 536870912 | bytes 9699328 | tf_op jit(solution)/shard_map/ied,edf->ief/dot_general | solution.py:43
  73.6 2.9 %fusion.16 = bf16[64,2,2048]{2,0,1:T(8,128)(2,1)S(1)} fusion(f32[64,2,2048]{2,0,1:T(8,128)S(1)} %convolution_bitcast_fusion, bf16[64,2,1024]{2,0,1:T(8,128)(2,1)S(1)} %all_gather.18, bf16[2,2048,1024]{2,1,0:T(8,128)(2,1)S(1)} %copy-done.1), kind=kOutput, calls=%fused_computation.29 | convolution fusion | flops 542113792 | bytes 10223616 | tf_op jit(solution)/shard_map/ied,efd->ief/dot_general | solution.py:53
  76.5 3.5 %convolution_bitcast_fusion.3 = f32[64,2,1024]{2,0,1:T(8,128)} fusion(bf16[64,2,2048]{2,0,1:T(8,128)(2,1)S(1)} %fusion.16, bf16[2,1024,2048]{2,1,0:T(8,128)(2,1)S(1)} %bitcast.72), kind=kOutput, calls=%fused_computation.12 | convolution fusion | flops 536870912 | bytes 9437184 | tf_op jit(solution)/shard_map/ief,edf->ied/dot_general | solution.py:62
  80.1 5.8 %convolution_bitcast_fusion.2 = f32[64,2,1024]{2,0,1:T(8,128)} fusion(bf16[2,2048,1024]{2,1,0:T(8,128)(2,1)} %param.9, f32[64,2,2048]{2,0,1:T(8,128)S(1)} %convolution_bitcast_fusion), kind=kOutput, calls=%fused_computation.11 | convolution fusion | flops 539230208 | bytes 9961472 | tf_op jit(solution)/shard_map/ief,efd->ied/dot_general | solution.py:47
  85.9 7.7 %reduce-scatter.9.cloned.1.call-done = f32[64,2,512]{2,0,1:T(8,128)} async-done(((f32[64,2,1024]{2,0,1:T(8,128)}), f32[64,2,512]{2,0,1:T(8,128)}) %reduce-scatter.9.cloned.1.call-update) | async-done | bytes 262160 | tf_op jit(solution)/shard_map/reduce_scatter | solution.py:17
  93.6 1.0 convert_element_type.41
  94.6 0.8 copy.17
  95.3 5.6 %all-to-all-start.2 = ((bf16[64,2,512]{2,1,0:T(2,128)(2,1)}), bf16[64,2,512]{2,1,0:T(2,128)(2,1)S(1)}, u32[]{:S(2)}, u32[]{:S(2)}) async-start(bf16[64,2,512]{2,1,0:T(2,128)(2,1)} %copy.17), calls=%async_computation.5 | async-start | bytes 262144 | tf_op jit(solution)/shard_map/all_to_all | solution.py:20
  101.0 9.9 %reduce-scatter.11.cloned.1.call-done = f32[64,2,512]{2,0,1:T(8,128)} async-done(((f32[64,2,1024]{2,0,1:T(8,128)}), f32[64,2,512]{2,0,1:T(8,128)}) %reduce-scatter.11.cloned.1.call-update) | async-done | bytes 262160 | tf_op jit(solution)/shard_map/reduce_scatter | solution.py:17
  110.9 1.0 convert_element_type.43
  111.9 0.8 copy.19
  112.7 5.7 %all-to-all-start.3 = ((bf16[64,2,512]{2,1,0:T(2,128)(2,1)}), bf16[64,2,512]{2,1,0:T(2,128)(2,1)}, u32[]{:S(2)}, u32[]{:S(2)}) async-start(bf16[64,2,512]{2,1,0:T(2,128)(2,1)} %copy.19), calls=%async_computation.7 | async-start | bytes 262144 | tf_op jit(solution)/shard_map/all_to_all | solution.py:20
  118.4 0.1 copy.27
  118.5 0.1 all_to_all.63
  118.6 6.4 %all_gather.20 = bf16[4,32,1024]{2,1,0:T(8,128)(2,1)S(1)} all-gather(bf16[4,32,512]{2,1,0:T(8,128)(2,1)S(1)} %all_to_all.63), channel_id=1, replica_groups=mesh['dp'=16,'tensor'=2] {'tensor'}, dimensions={2}, use_global_device_ids=true | all-gather | bytes 393216 | tf_op jit(solution)/shard_map/all_gather | solution.py:21
  125.0 0.4 multiply_reduce_fusion.1
  125.4 4.9 %psum.15 = f32[4,32]{1,0:T(4,128)S(1)} all-reduce(f32[4,32]{1,0:T(4,128)S(1)} %get-tuple-element.8), channel_id=1, replica_groups=mesh['dp'=16,'tensor'=2] {'tensor'}, use_global_device_ids=true, to_apply=%region_12.0 | all-reduce | flops 128 | bytes 1024 | tf_op jit(solution)/shard_map/psum | solution.py:65
  130.3 1.7 copy.26
  132.0 1.0 all_to_all.67
  133.0 5.8 %all_gather.21 = bf16[4,32,1024]{2,1,0:T(8,128)(2,1)S(1)} all-gather(bf16[4,32,512]{2,1,0:T(8,128)(2,1)S(1)} %all_to_all.67), channel_id=1, replica_groups=mesh['dp'=16,'tensor'=2] {'tensor'}, dimensions={2}, use_global_device_ids=true | all-gather | bytes 393216 | tf_op jit(solution)/shard_map/all_gather | solution.py:21
  138.8 0.3 convolution_bitcast_fusion.6
  139.1 2.0 convolution_bitcast_fusion.4
  141.1 5.8 %convolution_convert_fusion.1 = bf16[2,1024,2048]{2,1,0:T(8,128)(2,1)} fusion(bf16[64,2,1024]{2,0,1:T(8,128)(2,1)S(1)} %all_gather.19, bf16[64,2,2048]{2,0,1:T(8,128)(2,1)S(1)} %fusion.16), kind=kOutput, calls=%fused_computation.3 | convolution fusion | flops 541065216 | bytes 9175040 | tf_op jit(solution)/shard_map/ied,ief->edf/dot_general | solution.py:58
  146.8 5.8 %convolution_convert_fusion = bf16[2,2048,1024]{2,1,0:T(8,128)(2,1)} fusion(bf16[64,2,1024]{2,0,1:T(8,128)(2,1)S(1)} %copy-done.4, f32[64,2,2048]{2,0,1:T(8,128)S(1)} %convolution_bitcast_fusion), kind=kOutput, calls=%fused_computation.2 | convolution fusion | flops 543424512 | bytes 9699328 | tf_op jit(solution)/shard_map/ief,ied->efd/dot_general | solution.py:55
  152.6 1.4 fusion.9
  154.0 1.3 fusion.2
  155.3 48.4 %all-gather.3.cloned.1.call-done = f32[32768,32]{0,1:T(8,128)} async-done(((f32[1024,32]{0,1:T(8,128)}), f32[32768,32]{0,1:T(8,128)}) %all-gather.3.cloned.1.call-update) | async-done | bytes 4194320 | tf_op jit(solution)/shard_map/all_gather | solution.py:78
  203.6 4.6 %copy.21 = f32[4,8,32,1024]{3,2,1,0:T(8,128)S(1)} copy(f32[4,8,32,1024]{3,1,2,0:T(8,128)} %bitcast.73) | data formatting | bytes 8388608
  208.3 1.3 bitcast_reduce_fusion
  (33 shorter events, 0.5 us)
Async XLA Ops:
  7.2 1.1 copy-start
  7.2 22.7 %reduce-scatter.5.cloned.1.call-start = ((), (), s32[]{:S(2)}) async-start(), calls=%async_computation.8 | async-start | bytes 786432 | tf_op jit(solution)/shard_map/reduce_scatter | solution.py:8
  12.3 35.0 %reduce-scatter.7.cloned.1.call-start = ((), (), s32[]{:S(2)}) async-start(), calls=%async_computation.9 | async-start | bytes 786432 | tf_op jit(solution)/shard_map/reduce_scatter | solution.py:8
  31.6 17.5 %all-to-all-start = ((bf16[4,32,512]{2,0,1:T(4,128)(2,1)}), bf16[4,32,512]{2,0,1:T(4,128)(2,1)S(1)}, u32[]{:S(2)}, u32[]{:S(2)}) async-start(bf16[4,32,512]{2,0,1:T(4,128)(2,1)} %copy.13), calls=%async_computation.1 | async-start | bytes 262144 | tf_op jit(solution)/shard_map/all_to_all | solution.py:11
  49.1 13.5 %all-to-all-start.1 = ((bf16[4,32,512]{2,0,1:T(4,128)(2,1)}), bf16[4,32,512]{2,0,1:T(4,128)(2,1)S(1)}, u32[]{:S(2)}, u32[]{:S(2)}) async-start(bf16[4,32,512]{2,0,1:T(4,128)(2,1)} %copy.15), calls=%async_computation.3 | async-start | bytes 262144 | tf_op jit(solution)/shard_map/all_to_all | solution.py:11
  54.7 38.9 %reduce-scatter.9.cloned.1.call-start = ((), (), s32[]{:S(2)}) async-start(), calls=%async_computation.10 | async-start | bytes 786432 | tf_op jit(solution)/shard_map/reduce_scatter | solution.py:17
  61.3 15.2 %copy-start.3 = (bf16[64,2,1024]{2,0,1:T(8,128)(2,1)}, bf16[64,2,1024]{2,0,1:T(8,128)(2,1)S(1)}, u32[]{:S(2)}) copy-start(bf16[64,2,1024]{2,0,1:T(8,128)(2,1)S(1)} %all_gather.18) | copy-start | bytes 786436
  62.7 10.9 %copy-start.1 = (bf16[2,2048,1024]{2,1,0:T(8,128)(2,1)S(1)}, bf16[2,2048,1024]{2,1,0:T(8,128)(2,1)}, u32[]{:S(2)}) copy-start(bf16[2,2048,1024]{2,1,0:T(8,128)(2,1)} %param.9) | copy-start | bytes 25165828
  62.7 13.8 %slice-start = ((s8[8388608]{0:T(1024)(128)(4,1)}), s8[4194304]{0:T(1024)(128)(4,1)S(1)}, s32[]{:S(2)}) async-start(s8[8388608]{0:T(1024)(128)(4,1)} %bitcast.71), calls=%async_computation.13 | async-start | bytes 8388608
  68.5 8.0 %slice-start.1 = ((s8[8388608]{0:T(1024)(128)(4,1)}), s8[4194304]{0:T(1024)(128)(4,1)S(1)}, s32[]{:S(2)}) async-start(s8[8388608]{0:T(1024)(128)(4,1)} %bitcast.71), calls=%async_computation.14 | async-start | bytes 8388608
  80.0 58.8 %copy-start.2 = (bf16[4,72,1024]{2,1,0:T(8,128)(2,1)S(1)}, bf16[4,72,1024]{2,1,0:T(8,128)(2,1)}, u32[]{:S(2)}) copy-start(bf16[4,72,1024]{2,1,0:T(8,128)(2,1)} %param.6) | copy-start | bytes 1769476
  80.0 30.9 %reduce-scatter.11.cloned.1.call-start = ((), (), s32[]{:S(2)}) async-start(), calls=%async_computation.11 | async-start | bytes 786432 | tf_op jit(solution)/shard_map/reduce_scatter | solution.py:17
  95.3 17.4 %all-to-all-start.2 = ((bf16[64,2,512]{2,1,0:T(2,128)(2,1)}), bf16[64,2,512]{2,1,0:T(2,128)(2,1)S(1)}, u32[]{:S(2)}, u32[]{:S(2)}) async-start(bf16[64,2,512]{2,1,0:T(2,128)(2,1)} %copy.17), calls=%async_computation.5 | async-start | bytes 262144 | tf_op jit(solution)/shard_map/all_to_all | solution.py:20
  112.7 17.6 %all-to-all-start.3 = ((bf16[64,2,512]{2,1,0:T(2,128)(2,1)}), bf16[64,2,512]{2,1,0:T(2,128)(2,1)}, u32[]{:S(2)}, u32[]{:S(2)}) async-start(bf16[64,2,512]{2,1,0:T(2,128)(2,1)} %copy.19), calls=%async_computation.7 | async-start | bytes 262144 | tf_op jit(solution)/shard_map/all_to_all | solution.py:20
  118.4 85.2 %all-gather.3.cloned.1.call-start = ((), (), s32[]{:S(2)}) async-start(), calls=%async_computation.12 | async-start | bytes 4325376 | tf_op jit(solution)/shard_map/all_gather | solution.py:78
  139.1 7.8 %copy-start.4 = (bf16[64,2,1024]{2,0,1:T(8,128)(2,1)S(1)}, bf16[64,2,1024]{2,0,1:T(8,128)(2,1)}, u32[]{:S(2)}) copy-start(bf16[64,2,1024]{2,0,1:T(8,128)(2,1)} %copy-done.3) | copy-start | bytes 786436
  141.0 11.6 %copy-start.5 = (bf16[1024,32]{0,1:T(8,128)(2,1)S(1)}, bf16[1024,32]{0,1:T(8,128)(2,1)}, u32[]{:S(2)}) copy-start(bf16[1024,32]{0,1:T(8,128)(2,1)} %param.7) | copy-start | bytes 196612
Sparse Core Ops, SparseCore 0:
  12.4 17.3 reduce-scatter.4
  32.7 14.6 reduce-scatter.6
  80.1 13.4 reduce-scatter.8
  96.3 14.6 reduce-scatter.10
  141.2 62.4 all-gather.2
